TPU v7x, 256 devices: a whole 4x4x8 slice. The times are simulated.
256 devices in a mesh: expert: 8 (over x, core), replica: 32 (over y, z).
Axes of the slice: x: 4, y: 4, z: 8, core: 2. Of those that a mesh axis runs over, the one named last changes fastest.
Arguments:
- tokens: bfloat16 [1536, 4096], P(('expert', 'replica')), may hold values from -6 to 6
- out_grad: bfloat16 [1536, 4096], P(('expert', 'replica')), may hold values from -2.5 to 2.5
- expert_ids: int32 [1536, 2], P(('expert', 'replica')), may hold values from 0 to 7, all different within a row; in each aligned block of 6 rows (0 to 5, 6 to 11, ...) at most 2 rows name the same one
- gates: float32 [1536, 2], P(('expert', 'replica')), may hold values from 0.1 to 1
- w_gate: bfloat16 [8, 7168, 4096], P('expert', 'replica'), may hold values from -0.09375 to 0.09375
- w_up: bfloat16 [8, 7168, 4096], P('expert', 'replica'), may hold values from -0.09375 to 0.09375
- w_down: bfloat16 [8, 7168, 4096], P('expert', 'replica'), may hold values from -0.0625 to 0.0625
Outputs:
- gate_grad: float32 [1536, 2], P(('expert', 'replica'))
- input_grad: bfloat16 [1536, 4096], P(('expert', 'replica'))
- grad_gate: bfloat16 [8, 7168, 4096], P('expert', 'replica')
- grad_up: bfloat16 [8, 7168, 4096], P('expert', 'replica')
- grad_down: bfloat16 [8, 7168, 4096], P('expert', 'replica')
Inputs may be any that keep to these rules, and one draw needn't show every extreme that they name: `expert_ids`: each row names 2 different experts; among the rows of one device no expert is named more than 2 times.
All inputs are finite; a program needn't handle non-finite values.
Results may differ from a plain program's by a relative error of at most 0.02.
Values may be sent and summed in bfloat16 or wider, within the bound.
No kernel may reach another device: no remote copies, remote signals or barrier semaphores. Data moves between devices by JAX's collectives and lax.ppermute only.
A program may use at most 128 MiB of HBM per device.

v0:
```python
import jax
import jax.numpy as jnp
from jax import lax
from jax.sharding import Mesh
from jax.sharding import PartitionSpec as P

REPLICA = ("replica_0", "replica_1")
EXPERT_REPLICA = ("expert", "replica_0", "replica_1")


def split_up(value, dim, peers):
    shape = value.shape
    tiles = value.reshape(*shape[:dim], peers, shape[dim] // peers, *shape[dim + 1 :])
    return jnp.moveaxis(tiles, dim, 0)


def sum_at_owner(value, axis, dim):
    peers = lax.axis_size(axis)
    tiles = lax.all_to_all(split_up(value, dim, peers), axis, 0, 0, tiled=True)
    return jnp.sum(tiles, axis=0)


def own_rows(terms, axes):
    running = terms.astype(jnp.bfloat16)
    for axis in axes:
        running = lax.psum_scatter(running, axis, scatter_dimension=0, tiled=True)
    return running.astype(jnp.float32)


def on_device(tokens, out_grad, expert_ids, gates, w_gate, w_up, w_down):
    token_count = tokens.shape[0]
    fan_out = expert_ids.shape[1]
    model_width = tokens.shape[1]
    owners = lax.axis_size("expert")
    capacity = max(2, 4 * token_count * fan_out // (3 * owners))
    slot_count = owners * capacity
    flat_ids = expert_ids.reshape(-1)
    sequence_pos = jnp.arange(token_count * fan_out, dtype=jnp.int32)
    earlier = sequence_pos[None, :] < sequence_pos[:, None]
    same_expert = flat_ids[:, None] == flat_ids[None, :]
    slot_rank = jnp.sum(jnp.logical_and(same_expert, earlier), axis=1)
    target = flat_ids * capacity + slot_rank
    token_hot = (target[:, None] == jnp.arange(slot_count, dtype=jnp.int32)[None, :]).astype(
        jnp.float32
    )
    token_hot = token_hot.reshape(token_count, fan_out, slot_count)
    dispatch = jnp.sum(token_hot, axis=1).astype(jnp.bfloat16)
    slot_gate = jnp.sum(token_hot * gates[:, :, None], axis=(0, 1)).reshape(owners, capacity)
    leading = (((0,), (0,)), ((), ()))
    contract = (((1,), (1,)), ((), ()))
    send_inputs = (
        lax.dot_general(dispatch, tokens, leading, preferred_element_type=jnp.float32)
        .astype(jnp.bfloat16)
        .reshape(owners, capacity, model_width)
    )
    send_grads = (
        lax.dot_general(dispatch, out_grad, leading, preferred_element_type=jnp.float32)
        .astype(jnp.bfloat16)
        .reshape(owners, capacity, model_width)
    )
    gate_weight = w_gate[0]
    up_weight = w_up[0]
    down_weight = w_down[0]
    owned = (
        lax.all_to_all(send_inputs, "expert", split_axis=0, concat_axis=0, tiled=True),
        lax.all_to_all(send_grads, "expert", split_axis=0, concat_axis=0, tiled=True),
        lax.all_to_all(
            slot_gate.astype(jnp.bfloat16), "expert", split_axis=0, concat_axis=0, tiled=True
        ).astype(slot_gate.dtype),
    )
    column_inputs, column_grads, column_gates = (
        lax.all_gather(owned[0], REPLICA, axis=0, tiled=True),
        lax.all_gather(owned[1], REPLICA, axis=0, tiled=True),
        lax.all_gather(owned[2].astype(jnp.bfloat16), REPLICA, axis=0, tiled=True).astype(
            jnp.float32
        ),
    )
    gathered = column_inputs.reshape(-1, model_width)
    gate_pre = lax.dot_general(gathered, gate_weight, contract, preferred_element_type=jnp.float32)
    up_pre = lax.dot_general(gathered, up_weight, contract, preferred_element_type=jnp.float32)
    sigmoid_gate = jax.nn.sigmoid(gate_pre)
    active = gate_pre * sigmoid_gate
    hidden = (active * up_pre).astype(jnp.bfloat16)
    gathered_grad = column_grads.reshape(-1, model_width)
    row_gates = column_gates.reshape(-1)
    full_out = jnp.dot(hidden, down_weight, preferred_element_type=jnp.float32)
    partial_value = jnp.sum(gathered_grad * full_out, axis=1)
    summed_products = sum_at_owner(partial_value, REPLICA, 0)
    returned = lax.all_to_all(
        summed_products.reshape(owners, capacity), "expert", split_axis=0, concat_axis=0, tiled=True
    )
    gate_grad = jnp.sum(token_hot * returned.reshape(-1)[None, None, :], axis=2)
    scaled = (row_gates[:, None] * gathered_grad).astype(jnp.bfloat16)
    hidden_grad = lax.dot_general(scaled, down_weight, contract, preferred_element_type=jnp.float32)
    gate_pre_grad = (
        hidden_grad * up_pre * sigmoid_gate * (1.0 + gate_pre * (1.0 - sigmoid_gate))
    ).astype(jnp.bfloat16)
    up_pre_grad = (hidden_grad * active).astype(jnp.bfloat16)
    grad_down = lax.dot_general(hidden, scaled, leading, preferred_element_type=jnp.float32).astype(
        jnp.bfloat16
    )
    grad_gate = lax.dot_general(
        gate_pre_grad, gathered, leading, preferred_element_type=jnp.float32
    ).astype(jnp.bfloat16)
    grad_up = lax.dot_general(
        up_pre_grad, gathered, leading, preferred_element_type=jnp.float32
    ).astype(jnp.bfloat16)
    slot_grad = own_rows(
        jnp.dot(gate_pre_grad, gate_weight, preferred_element_type=jnp.float32)
        + jnp.dot(up_pre_grad, up_weight, preferred_element_type=jnp.float32),
        REPLICA,
    ).astype(jnp.bfloat16)
    slot_back = lax.all_to_all(
        slot_grad.reshape(owners, capacity, model_width),
        "expert",
        split_axis=0,
        concat_axis=0,
        tiled=True,
    )
    slot_back = slot_back.reshape(slot_count, model_width)
    input_grad = jnp.dot(dispatch, slot_back, preferred_element_type=jnp.float32).astype(
        jnp.bfloat16
    )
    return (gate_grad, input_grad, grad_gate[None], grad_up[None], grad_down[None])


def solution(mesh):
    torus = Mesh(
        mesh.devices.reshape(mesh.shape["expert"], 4, 8), ("expert", "replica_0", "replica_1")
    )
    in_specs = (
        P(EXPERT_REPLICA, None),
        P(EXPERT_REPLICA, None),
        P(EXPERT_REPLICA, None),
        P(EXPERT_REPLICA, None),
        P("expert", REPLICA, None),
        P("expert", REPLICA, None),
        P("expert", REPLICA, None),
    )
    out_specs = (
        P(EXPERT_REPLICA, None),
        P(EXPERT_REPLICA, None),
        P("expert", REPLICA, None),
        P("expert", REPLICA, None),
        P("expert", REPLICA, None),
    )
    return jax.shard_map(
        on_device, mesh=torus, in_specs=in_specs, out_specs=out_specs, check_vma=False
    )
```

profile of v0, /device:TPU:1, one launch (start us, length us, event | category | flops | bytes accessed | tf_op | source)
XLA Modules:
  0.0 404.9 jit_solution(4118786558378128443)
XLA Ops:
  7.2 0.9 copy.30
  8.6 1.1 convolution_convert_fusion.3
  9.8 11.5 %all_to_all.42 = bf16[8,2,4096]{2,1,0:T(2,128)(2,1)} all-to-all(bf16[8,2,4096]{2,1,0:T(2,128)(2,1)S(1)} %reshape.81), channel_id=1, replica_groups=mesh['expert'=8,'replica_0'=4,'replica_1'=8] {'expert'}, dimensions={0} | all-to-all | bytes 262144 | tf_op jit(solution)/shard_map/all_to_all | solution.py:65
  21.3 1.1 convolution_convert_fusion.4
  22.5 9.2 %all_to_all.43 = bf16[8,2,4096]{2,1,0:T(2,128)(2,1)} all-to-all(bf16[8,2,4096]{2,1,0:T(2,128)(2,1)S(1)} %reshape.80), channel_id=1, replica_groups=mesh['expert'=8,'replica_0'=4,'replica_1'=8] {'expert'}, dimensions={0} | all-to-all | bytes 262144 | tf_op jit(solution)/shard_map/all_to_all | solution.py:66
  31.7 68.7 %all-gather.6.cloned.1.call-done = bf16[256,2,4096]{2,1,0:T(2,128)(2,1)} async-done(((bf16[8,2,4096]{2,1,0:T(2,128)(2,1)}), bf16[256,2,4096]{2,1,0:T(2,128)(2,1)}) %all-gather.6.cloned.1.call-update) | async-done | bytes 4194320 | tf_op jit(solution)/shard_map/all_gather | solution.py:72
  100.4 7.2 %reshape.82 = bf16[512,4096]{1,0:T(8,128)(2,1)} reshape(bf16[256,2,4096]{2,1,0:T(2,128)(2,1)} %all-gather.6.cloned.1.call-done) | data formatting | bytes 8388608 | tf_op jit(solution)/shard_map/reshape | solution.py:78
  107.6 4.3 %fusion.12 = f32[512,224]{0,1:T(8,128)S(1)} fusion(bf16[512,4096]{1,0:T(8,128)(2,1)} %reshape.82, bf16[1,224,4096]{2,1,0:T(8,128)(2,1)} %param.11), kind=kOutput, calls=%fused_computation.22 | convolution fusion | flops 939524096 | bytes 6488064 | tf_op jit(solution)/shard_map/dot_general | solution.py:79
  112.0 2.3 multiply_convert_fusion.5
  114.3 67.3 %all-gather.4.cloned.1.call-done = bf16[256,2,4096]{2,1,0:T(2,128)(2,1)} async-done(((bf16[8,2,4096]{2,1,0:T(2,128)(2,1)}), bf16[256,2,4096]{2,1,0:T(2,128)(2,1)}) %all-gather.4.cloned.1.call-update) | async-done | bytes 4194320 | tf_op jit(solution)/shard_map/all_gather | solution.py:73
  181.6 7.6 %reshape.85 = f32[512,4096]{1,0:T(8,128)} reshape(bf16[256,2,4096]{2,1,0:T(2,128)(2,1)} %all-gather.4.cloned.1.call-done) | data formatting | bytes 12582912 | tf_op jit(solution)/shard_map/convert_element_type | solution.py:87
  189.2 5.3 %multiply_reduce_fusion = f32[512]{0:T(512)S(1)} fusion(f32[512,4096]{1,0:T(8,128)} %reshape.85, bf16[512,224]{0,1:T(8,128)(2,1)S(1)} %get-tuple-element.14, bf16[1,224,4096]{2,1,0:T(8,128)(2,1)} %param.13), kind=kOutput, calls=%fused_computation.3 | convolution fusion | flops 943717888 | bytes 10455040 | tf_op jit(solution)/shard_map/dot_general | solution.py:86
  194.6 14.5 %all_to_all.44 = f32[32,1,16]{2,1,0:T(1,128)S(1)} all-to-all(f32[32,1,16]{2,1,0:T(1,128)S(1)} %bitcast.46), channel_id=1, replica_groups=mesh['expert'=8,'replica_0'=4,'replica_1'=8] {'replica_0','replica_1'}, dimensions={0} | all-to-all | bytes 4096 | tf_op jit(solution)/shard_map/all_to_all | solution.py:19
  209.1 0.7 all_to_all.31
  209.8 8.9 %all-to-all-start.3 = ((f32[8,1,2]{2,1,0:T(1,128)}), f32[8,1,2]{2,1,0:T(1,128)S(1)}, u32[]{:S(2)}, u32[]{:S(2)}) async-start(f32[8,1,2]{2,1,0:T(1,128)} %bitcast.4), calls=%async_computation.3 | async-start | bytes 8192 | tf_op jit(solution)/shard_map/all_to_all | solution.py:89
  218.8 4.4 %all-to-all-done.3 = f32[8,1,2]{2,1,0:T(1,128)S(1)} async-done(((f32[8,1,2]{2,1,0:T(1,128)}), f32[8,1,2]{2,1,0:T(1,128)S(1)}, u32[]{:S(2)}, u32[]{:S(2)}) %all-to-all-start.3) | async-done | bytes 96 | tf_op jit(solution)/shard_map/all_to_all | solution.py:89
  224.8 7.6 %all_to_all.45 = bf16[8,1,2]{2,1,0:T(2,128)(2,1)S(1)} all-to-all(bf16[8,1,2]{2,1,0:T(2,128)(2,1)S(1)} %convert_element_type.102), channel_id=1, replica_groups=mesh['expert'=8,'replica_0'=4,'replica_1'=8] {'expert'}, dimensions={0} | all-to-all | bytes 64 | tf_op jit(solution)/shard_map/all_to_all | solution.py:67
  232.4 31.3 %all-gather = bf16[256,1,2]{2,1,0:T(2,128)(2,1)S(1)} all-gather(bf16[8,1,2]{2,1,0:T(2,128)(2,1)S(1)} %all_to_all.45), channel_id=2, replica_groups=mesh['expert'=8,'replica_0'=4,'replica_1'=8] {'replica_0','replica_1'}, dimensions={0}, use_global_device_ids=true | all-gather | bytes 1056 | tf_op jit(solution)/shard_map/all_gather | solution.py:74
  263.8 10.4 %multiply_convert_fusion.1 = bf16[256,2,4096]{2,1,0:T(2,128)(2,1)} fusion(f32[256,2]{1,0:T(8,128)S(1)} %bitcast.45, bf16[256,2,4096]{2,1,0:T(2,128)(2,1)} %all-gather.4.cloned.1.call-done), kind=kLoop, calls=%fused_computation.2 | loop fusion | flops 6291456 | bytes 8390656 | tf_op jit(solution)/shard_map/convert_element_type | solution.py:93
  274.2 7.2 %convert_element_type.91 = bf16[512,4096]{1,0:T(8,128)(2,1)} reshape(bf16[256,2,4096]{2,1,0:T(2,128)(2,1)} %multiply_convert_fusion.1) | data formatting | bytes 8388608 | tf_op jit(solution)/shard_map/convert_element_type | solution.py:93
  281.4 4.4 %multiply_convert_fusion.3 = (bf16[512,224]{0,1:T(8,128)(2,1)S(1)}, bf16[512,224]{0,1:T(8,128)(2,1)S(1)}) fusion(f32[512,224]{0,1:T(8,128)S(1)} %fusion.12, f32[512,224]{0,1:T(8,128)} %get-tuple-element.15, bf16[512,4096]{1,0:T(8,128)(2,1)} %convert_element_type.91, bf16[1,224,4096]{2,1,0:T(8,128)(2,1)} %param.13), kind=kOutput, calls=%fused_computation.24 | convolution fusion | flops 941015040 | bytes 7405568 | tf_op jit(solution)/shard_map/dot_general | solution.py:94
  285.8 1.3 fusion.10
  287.1 3.3 add_convert_fusion
  290.7 53.7 %reduce-scatter.3.cloned.1.call-done = bf16[128,4096]{1,0:T(8,128)(2,1)} async-done(((bf16[512,4096]{1,0:T(8,128)(2,1)}), bf16[128,4096]{1,0:T(8,128)(2,1)}) %reduce-scatter.3.cloned.1.call-update) | async-done | bytes 1048592 | tf_op jit(solution)/shard_map/reduce_scatter | solution.py:26
  345.6 4.5 %fusion.1 = bf16[1,224,4096]{2,1,0:T(8,128)(2,1)} fusion(bf16[512,224]{0,1:T(8,128)(2,1)S(1)} %get-tuple-element.12, bf16[512,4096]{1,0:T(8,128)(2,1)} %reshape.82), kind=kOutput, calls=%fused_computation.8 | convolution fusion | flops 940441600 | bytes 6258688 | tf_op jit(solution)/shard_map/dot_general | solution.py:105
  350.2 5.8 %fusion.2 = bf16[1,224,4096]{2,1,0:T(8,128)(2,1)} fusion(bf16[512,224]{0,1:T(8,128)(2,1)S(1)} %get-tuple-element.14, f32[512,4096]{1,0:T(8,128)} %reshape.85, f32[512]{0:T(512)S(1)} %mul.80), kind=kOutput, calls=%fused_computation.9 | convolution fusion | flops 944635904 | bytes 10455040 | tf_op jit(solution)/shard_map/dot_general | solution.py:99
  356.0 24.6 %reduce-scatter.5.cloned.1.call-done = bf16[16,4096]{1,0:T(8,128)(2,1)} async-done(((bf16[128,4096]{1,0:T(8,128)(2,1)}), bf16[16,4096]{1,0:T(8,128)(2,1)}) %reduce-scatter.5.cloned.1.call-update) | async-done | bytes 131088 | tf_op jit(solution)/shard_map/reduce_scatter | solution.py:26
  380.6 1.6 reshape.83
  382.3 10.0 %all-to-all-start.5 = ((bf16[8,2,4096]{2,1,0:T(2,128)(2,1)}), bf16[8,2,4096]{2,1,0:T(2,128)(2,1)S(1)}, u32[]{:S(2)}, u32[]{:S(2)}) async-start(bf16[8,2,4096]{2,1,0:T(2,128)(2,1)} %reshape.83), calls=%async_computation.7 | async-start | bytes 262144 | tf_op jit(solution)/shard_map/all_to_all | solution.py:113
  392.3 4.5 %fusion = bf16[1,224,4096]{2,1,0:T(8,128)(2,1)} fusion(bf16[512,224]{0,1:T(8,128)(2,1)S(1)} %get-tuple-element.13, bf16[512,4096]{1,0:T(8,128)(2,1)} %reshape.82), kind=kOutput, calls=%fused_computation.7 | convolution fusion | flops 940441600 | bytes 6258688 | tf_op jit(solution)/shard_map/dot_general | solution.py:102
  396.8 0.7 all-to-all-done.5
  397.6 0.8 convolution_convert_fusion.5
  (36 shorter events, 4.1 us)
Async XLA Ops:
  7.2 104.8 %copy-start = (bf16[1,224,4096]{2,1,0:T(8,128)(2,1)S(1)}, bf16[1,224,4096]{2,1,0:T(8,128)(2,1)}, u32[]{:S(2)}) copy-start(bf16[1,224,4096]{2,1,0:T(8,128)(2,1)} %param.12) | copy-start | bytes 5505028
  7.2 93.2 %all-gather.6.cloned.1.call-start = ((), (), s32[]{:S(2)}) async-start(), calls=%async_computation.9 | async-start | bytes 4325376 | tf_op jit(solution)/shard_map/all_gather | solution.py:72
  21.3 160.3 %all-gather.4.cloned.1.call-start = ((), (), s32[]{:S(2)}) async-start(), calls=%async_computation.8 | async-start | bytes 4325376 | tf_op jit(solution)/shard_map/all_gather | solution.py:73
  107.6 4.4 %copy-start.1 = (bf16[512,4096]{1,0:T(8,128)(2,1)S(1)}, bf16[512,4096]{1,0:T(8,128)(2,1)}, u32[]{:S(2)}) copy-start(bf16[512,4096]{1,0:T(8,128)(2,1)} %reshape.82) | copy-start | bytes 12582916
  189.2 29.6 %copy-start.3 = (f32[6,2]{0,1:T(2,128)S(1)}, f32[6,2]{0,1:T(2,128)}, u32[]{:S(2)}) copy-start(f32[6,2]{0,1:T(2,128)} %param.10) | copy-start | bytes 148
  209.8 13.5 %all-to-all-start.3 = ((f32[8,1,2]{2,1,0:T(1,128)}), f32[8,1,2]{2,1,0:T(1,128)S(1)}, u32[]{:S(2)}, u32[]{:S(2)}) async-start(f32[8,1,2]{2,1,0:T(1,128)} %bitcast.4), calls=%async_computation.3 | async-start | bytes 8192 | tf_op jit(solution)/shard_map/all_to_all | solution.py:89
  218.7 125.7 %reduce-scatter.3.cloned.1.call-start = ((), (), s32[]{:S(2)}) async-start(), calls=%async_computation.10 | async-start | bytes 5242880 | tf_op jit(solution)/shard_map/reduce_scatter | solution.py:26
  281.4 4.4 %copy-start.2 = (bf16[1,224,4096]{2,1,0:T(8,128)(2,1)S(1)}, bf16[1,224,4096]{2,1,0:T(8,128)(2,1)}, u32[]{:S(2)}) copy-start(bf16[1,224,4096]{2,1,0:T(8,128)(2,1)} %param.11) | copy-start | bytes 5505028
  290.5 90.2 %reduce-scatter.5.cloned.1.call-start = ((), (), s32[]{:S(2)}) async-start(), calls=%async_computation.11 | async-start | bytes 1179648 | tf_op jit(solution)/shard_map/reduce_scatter | solution.py:26
  382.3 15.3 %all-to-all-start.5 = ((bf16[8,2,4096]{2,1,0:T(2,128)(2,1)}), bf16[8,2,4096]{2,1,0:T(2,128)(2,1)S(1)}, u32[]{:S(2)}, u32[]{:S(2)}) async-start(bf16[8,2,4096]{2,1,0:T(2,128)(2,1)} %reshape.83), calls=%async_computation.7 | async-start | bytes 262144 | tf_op jit(solution)/shard_map/all_to_all | solution.py:113
Sparse Core Ops, SparseCore 0:
  21.4 78.9 all-gather.5
  103.0 78.5 all-gather.3
  290.6 53.7 reduce-scatter.2
  346.8 33.7 reduce-scatter.4
where the time goes:
time: 406 us; the launch traced here: 405 us
  waiting for transfers between devices  220 us (54%)
  blocking collectives  74 us (18%)
  matrix products  38.8 us (10%)
  local copies, waits for them, and re-layouts  27.3 us (7%)
  starting transfers between devices  19.3 us (5%)
  between operations  13.9 us (3%)
  other arithmetic  12.1 us (3%)
    reduce_scatter x2, waiting for transfers between devices, own_rows(): running = lax.psum_scatter(running, axis, scatter_dimension=0, tiled=True)  78.3 us
    all_gather x1, waiting for transfers between devices, on_device(): lax.all_gather(owned[0], REPLICA, axis=0, tiled=True)  68.7 us
    all_gather x1, waiting for transfers between devices, on_device(): lax.all_gather(owned[1], REPLICA, axis=0, tiled=True)  67.3 us
    all_gather x1, blocking collectives, on_device(): lax.all_gather(owned[2].astype(jnp.bfloat16), REPLICA, axis=0, tiled=True)  31.3 us
    all_to_all x1, blocking collectives, sum_at_owner(): tiles = lax.all_to_all(split_up(value, dim, peers), axis, 0, 0, tiled=True)  14.5 us
    all_to_all x1, blocking collectives, on_device(): lax.all_to_all(send_inputs, 'expert', split_axis=0, concat_axis=0, tiled=...  11.5 us
    convert_element_type x1, other arithmetic, on_device(): scaled = (row_gates[:, None] * gathered_grad).astype(jnp.bfloat16)  10.4 us
    all_to_all x1, starting transfers between devices, on_device(): lax.all_to_all(slot_grad.reshape(owners, capacity, model_width), 'expert'...  10 us
  transfers between devices with their start and end apart: 6, of which 6 were waited for; matrix products, arithmetic and copies ran while one was open for 8% of the time, Pallas kernels for 0%

commit v1 on v0

--- a/solution.py
+++ b/solution.py
@@ -69,7 +69,9 @@
         ).astype(slot_gate.dtype),
     )
     column_inputs, column_grads, column_gates = (
-        lax.all_gather(owned[0], REPLICA, axis=0, tiled=True),
+        jnp.concatenate(
+            lax.all_to_all(jnp.stack([owned[0]] * lax.axis_size(REPLICA)), REPLICA, 0, 0), axis=0
+        ),
         lax.all_gather(owned[1], REPLICA, axis=0, tiled=True),
         lax.all_gather(owned[2].astype(jnp.bfloat16), REPLICA, axis=0, tiled=True).astype(
             jnp.float32

time: 406 us -> 397 us (0.978)
  waiting for transfers between devices: 220 us -> 194 us
  starting transfers between devices: 19.3 us -> 32.3 us
  local copies, waits for them, and re-layouts: 27.3 us -> 34.2 us
    all_to_all x0 -> x2, waiting for transfers between devices: none -> 108 us  [the longest x1 104 us: on_device(): lax.all_to_all(jnp.stack([owned[0]] * lax.axis_size(REPLICA)), REPLICA, 0...]
    all_gather x1 -> x0, waiting for transfers between devices: 68.7 us -> none  [on_device(): lax.all_gather(owned[0], REPLICA, axis=0, tiled=True)]
    all_gather x1, waiting for transfers between devices: 67.3 us -> 0.75 us  [on_device(): lax.all_gather(owned[1], REPLICA, axis=0, tiled=True)]
    all_to_all x0 -> x2, starting transfers between devices: none -> 17.1 us  [the longest x1 10.6 us: on_device(): lax.all_to_all(jnp.stack([owned[0]] * lax.axis_size(REPLICA)), REPLICA, 0...]
    another operation x0 -> x2, local copies, waits for them, and re-layouts: none -> 13.4 us  [the longest x1 7.22 us: on_device(): gathered = column_inputs.reshape(-1, model_width)]
    all_to_all x1 -> x0, blocking collectives: 11.5 us -> none  [on_device(): lax.all_to_all(send_inputs, 'expert', split_axis=0, concat_axis=0, tiled=...]
    all_to_all x1, blocking collectives: 14.5 us -> 23.1 us  [sum_at_owner(): tiles = lax.all_to_all(split_up(value, dim, peers), axis, 0, 0, tiled=True)]
    reshape x1 -> x0, local copies, waits for them, and re-layouts: 7.22 us -> none  [on_device(): gathered = column_inputs.reshape(-1, model_width)]
  transfers between devices with their start and end apart: 6 -> 7, of which waited for: 6 -> 7; matrix products, arithmetic and copies ran while one was open for 8% -> 8% of each run, Pallas kernels for 0% -> 0%
where the time goes in v1:
time: 397 us; the launch traced here: 396 us
  waiting for transfers between devices  194 us (49%)
  blocking collectives  71.1 us (18%)
  matrix products  38.9 us (10%)
  local copies, waits for them, and re-layouts  34.2 us (9%)
  starting transfers between devices  32.3 us (8%)
  between operations  13.9 us (4%)
  other arithmetic  12.1 us (3%)
    all_to_all x1, waiting for transfers between devices, on_device(): lax.all_to_all(jnp.stack([owned[0]] * lax.axis_size(REPLICA)), REPLICA, 0...  104 us
    reduce_scatter x2, waiting for transfers between devices, own_rows(): running = lax.psum_scatter(running, axis, scatter_dimension=0, tiled=True)  79 us
    all_gather x1, blocking collectives, on_device(): lax.all_gather(owned[2].astype(jnp.bfloat16), REPLICA, axis=0, tiled=True)  31.3 us
    all_to_all x1, blocking collectives, sum_at_owner(): tiles = lax.all_to_all(split_up(value, dim, peers), axis, 0, 0, tiled=True)  23.1 us
    all_to_all x1, starting transfers between devices, on_device(): lax.all_to_all(jnp.stack([owned[0]] * lax.axis_size(REPLICA)), REPLICA, 0...  10.6 us
    convert_element_type x1, other arithmetic, on_device(): scaled = (row_gates[:, None] * gathered_grad).astype(jnp.bfloat16)  10.4 us
    all_to_all x1, starting transfers between devices, on_device(): lax.all_to_all(slot_grad.reshape(owners, capacity, model_width), 'expert'...  9.51 us
    all_to_all x1, blocking collectives, on_device(): lax.all_to_all(send_grads, 'expert', split_axis=0, concat_axis=0, tiled=T...  9.15 us
  transfers between devices with their start and end apart: 7, of which 7 were waited for; matrix products, arithmetic and copies ran while one was open for 8% of the time, Pallas kernels for 0%

profile of v1, /device:TPU:1, one launch (start us, length us, event | category | flops | bytes accessed | tf_op | source)
XLA Modules:
  0.0 396.1 jit_solution(1610069984219690643)
XLA Ops:
  7.2 0.9 copy.30
  8.5 1.1 convolution_convert_fusion.3
  10.4 6.5 %all-to-all-start.1 = ((bf16[8,2,4096]{2,1,0:T(2,128)(2,1)}), bf16[8,2,4096]{2,1,0:T(2,128)(2,1)S(1)}, u32[]{:S(2)}, u32[]{:S(2)}) async-start(bf16[8,2,4096]{2,1,0:T(2,128)(2,1)} %reshape.80), calls=%async_computation.1 | async-start | bytes 262144 | tf_op jit(solution)/shard_map/all_to_all | solution.py:65
  16.8 1.1 convolution_convert_fusion.4
  18.0 4.1 %all-to-all-done.1 = bf16[8,2,4096]{2,1,0:T(2,128)(2,1)S(1)} async-done(((bf16[8,2,4096]{2,1,0:T(2,128)(2,1)}), bf16[8,2,4096]{2,1,0:T(2,128)(2,1)S(1)}, u32[]{:S(2)}, u32[]{:S(2)}) %all-to-all-start.1) | async-done | bytes 131104 | tf_op jit(solution)/shard_map/all_to_all | solution.py:65
  22.1 9.2 %all_to_all.47 = bf16[8,2,4096]{2,1,0:T(2,128)(2,1)} all-to-all(bf16[8,2,4096]{2,1,0:T(2,128)(2,1)S(1)} %reshape.79), channel_id=1, replica_groups=mesh['expert'=8,'replica_0'=4,'replica_1'=8] {'expert'}, dimensions={0} | all-to-all | bytes 262144 | tf_op jit(solution)/shard_map/all_to_all | solution.py:66
  31.3 6.2 %stack.2 = bf16[32,8,2,4096]{3,2,1,0:T(2,128)(2,1)} broadcast(bf16[8,2,4096]{2,1,0:T(2,128)(2,1)S(1)} %all-to-all-done.1), dimensions={1,2,3} | broadcast | bytes 4325376 | tf_op jit(solution)/shard_map/stack | solution.py:73
  37.5 10.6 %all-to-all-start.2 = ((bf16[32,8,2,4096]{3,2,1,0:T(2,128)(2,1)}), bf16[32,8,2,4096]{3,2,1,0:T(2,128)(2,1)}, u32[]{:S(2)}, u32[]{:S(2)}) async-start(bf16[32,8,2,4096]{3,2,1,0:T(2,128)(2,1)} %stack.2), calls=%async_computation.2 | async-start | bytes 8388608 | tf_op jit(solution)/shard_map/all_to_all | solution.py:73
  48.8 104.0 %all-to-all-done.2 = bf16[32,8,2,4096]{3,2,1,0:T(2,128)(2,1)} async-done(((bf16[32,8,2,4096]{3,2,1,0:T(2,128)(2,1)}), bf16[32,8,2,4096]{3,2,1,0:T(2,128)(2,1)}, u32[]{:S(2)}, u32[]{:S(2)}) %all-to-all-start.2) | async-done | bytes 4194336 | tf_op jit(solution)/shard_map/all_to_all | solution.py:73
  152.9 7.2 %reshape_reshape.3 = bf16[512,4096]{1,0:T(8,128)(2,1)} reshape(bf16[32,8,2,4096]{3,2,1,0:T(2,128)(2,1)} %all-to-all-done.2) | data formatting | bytes 8388608 | tf_op jit(solution)/shard_map/reshape;reshape | solution.py:80
  160.1 4.4 %fusion.12 = f32[512,224]{0,1:T(8,128)S(1)} fusion(bf16[512,4096]{1,0:T(8,128)(2,1)} %reshape_reshape.3, bf16[1,224,4096]{2,1,0:T(8,128)(2,1)} %param.11), kind=kOutput, calls=%fused_computation.22 | convolution fusion | flops 939524096 | bytes 6488064 | tf_op jit(solution)/shard_map/dot_general | solution.py:81
  164.5 2.3 multiply_convert_fusion.5
  167.5 7.6 %reshape.83 = f32[512,4096]{1,0:T(8,128)} reshape(bf16[256,2,4096]{2,1,0:T(2,128)(2,1)} %all-gather.3.cloned.1.call-done) | data formatting | bytes 12582912 | tf_op jit(solution)/shard_map/convert_element_type | solution.py:89
  175.1 5.3 %multiply_reduce_fusion = f32[512]{0:T(512)S(1)} fusion(f32[512,4096]{1,0:T(8,128)} %reshape.83, bf16[512,224]{0,1:T(8,128)(2,1)S(1)} %get-tuple-element.14, bf16[1,224,4096]{2,1,0:T(8,128)(2,1)} %param.13), kind=kOutput, calls=%fused_computation.3 | convolution fusion | flops 943717888 | bytes 10455040 | tf_op jit(solution)/shard_map/dot_general | solution.py:88
  180.5 23.1 %all_to_all.48 = f32[32,1,16]{2,1,0:T(1,128)S(1)} all-to-all(f32[32,1,16]{2,1,0:T(1,128)S(1)} %bitcast.46), channel_id=1, replica_groups=mesh['expert'=8,'replica_0'=4,'replica_1'=8] {'replica_0','replica_1'}, dimensions={0} | all-to-all | bytes 4096 | tf_op jit(solution)/shard_map/all_to_all | solution.py:19
  204.4 5.4 %all-to-all-start.4 = ((f32[8,1,2]{2,1,0:T(1,128)}), f32[8,1,2]{2,1,0:T(1,128)S(1)}, u32[]{:S(2)}, u32[]{:S(2)}) async-start(f32[8,1,2]{2,1,0:T(1,128)} %bitcast.4), calls=%async_computation.4 | async-start | bytes 8192 | tf_op jit(solution)/shard_map/all_to_all | solution.py:91
  209.9 4.4 %all-to-all-done.4 = f32[8,1,2]{2,1,0:T(1,128)S(1)} async-done(((f32[8,1,2]{2,1,0:T(1,128)}), f32[8,1,2]{2,1,0:T(1,128)S(1)}, u32[]{:S(2)}, u32[]{:S(2)}) %all-to-all-start.4) | async-done | bytes 96 | tf_op jit(solution)/shard_map/all_to_all | solution.py:91
  215.8 7.6 %all_to_all.49 = bf16[8,1,2]{2,1,0:T(2,128)(2,1)S(1)} all-to-all(bf16[8,1,2]{2,1,0:T(2,128)(2,1)S(1)} %convert_element_type.102), channel_id=1, replica_groups=mesh['expert'=8,'replica_0'=4,'replica_1'=8] {'expert'}, dimensions={0} | all-to-all | bytes 64 | tf_op jit(solution)/shard_map/all_to_all | solution.py:67
  223.5 31.3 %all-gather = bf16[256,1,2]{2,1,0:T(2,128)(2,1)S(1)} all-gather(bf16[8,1,2]{2,1,0:T(2,128)(2,1)S(1)} %all_to_all.49), channel_id=2, replica_groups=mesh['expert'=8,'replica_0'=4,'replica_1'=8] {'replica_0','replica_1'}, dimensions={0}, use_global_device_ids=true | all-gather | bytes 1056 | tf_op jit(solution)/shard_map/all_gather | solution.py:76
  254.9 10.4 %multiply_convert_fusion.1 = bf16[256,2,4096]{2,1,0:T(2,128)(2,1)} fusion(f32[256,2]{1,0:T(8,128)S(1)} %bitcast.45, bf16[256,2,4096]{2,1,0:T(2,128)(2,1)} %all-gather.3.cloned.1.call-done), kind=kLoop, calls=%fused_computation.2 | loop fusion | flops 6291456 | bytes 8390656 | tf_op jit(solution)/shard_map/convert_element_type | solution.py:95
  265.2 7.2 %convert_element_type.91 = bf16[512,4096]{1,0:T(8,128)(2,1)} reshape(bf16[256,2,4096]{2,1,0:T(2,128)(2,1)} %multiply_convert_fusion.1) | data formatting | bytes 8388608 | tf_op jit(solution)/shard_map/convert_element_type | solution.py:95
  272.4 4.4 %multiply_convert_fusion.3 = (bf16[512,224]{0,1:T(8,128)(2,1)S(1)}, bf16[512,224]{0,1:T(8,128)(2,1)S(1)}) fusion(f32[512,224]{0,1:T(8,128)S(1)} %fusion.12, f32[512,224]{0,1:T(8,128)} %get-tuple-element.15, bf16[512,4096]{1,0:T(8,128)(2,1)} %convert_element_type.91, bf16[1,224,4096]{2,1,0:T(8,128)(2,1)} %param.13), kind=kOutput, calls=%fused_computation.24 | convolution fusion | flops 941015040 | bytes 7405568 | tf_op jit(solution)/shard_map/dot_general | solution.py:96
  276.9 1.3 fusion.10
  278.2 3.3 add_convert_fusion
  281.8 53.7 %reduce-scatter.3.cloned.1.call-done = bf16[128,4096]{1,0:T(8,128)(2,1)} async-done(((bf16[512,4096]{1,0:T(8,128)(2,1)}), bf16[128,4096]{1,0:T(8,128)(2,1)}) %reduce-scatter.3.cloned.1.call-update) | async-done | bytes 1048592 | tf_op jit(solution)/shard_map/reduce_scatter | solution.py:26
  336.7 4.5 %fusion.1 = bf16[1,224,4096]{2,1,0:T(8,128)(2,1)} fusion(bf16[512,224]{0,1:T(8,128)(2,1)S(1)} %get-tuple-element.12, bf16[512,4096]{1,0:T(8,128)(2,1)} %reshape_reshape.3), kind=kOutput, calls=%fused_computation.8 | convolution fusion | flops 940441600 | bytes 6258688 | tf_op jit(solution)/shard_map/dot_general | solution.py:107
  341.2 5.8 %fusion.2 = bf16[1,224,4096]{2,1,0:T(8,128)(2,1)} fusion(bf16[512,224]{0,1:T(8,128)(2,1)S(1)} %get-tuple-element.14, f32[512,4096]{1,0:T(8,128)} %reshape.83, f32[512]{0:T(512)S(1)} %mul.80), kind=kOutput, calls=%fused_computation.9 | convolution fusion | flops 944635904 | bytes 10455040 | tf_op jit(solution)/shard_map/dot_general | solution.py:101
  347.1 25.3 %reduce-scatter.5.cloned.1.call-done = bf16[16,4096]{1,0:T(8,128)(2,1)} async-done(((bf16[128,4096]{1,0:T(8,128)(2,1)}), bf16[16,4096]{1,0:T(8,128)(2,1)}) %reduce-scatter.5.cloned.1.call-update) | async-done | bytes 131088 | tf_op jit(solution)/shard_map/reduce_scatter | solution.py:26
  372.3 1.6 reshape.81
  374.0 9.5 %all-to-all-start.6 = ((bf16[8,2,4096]{2,1,0:T(2,128)(2,1)}), bf16[8,2,4096]{2,1,0:T(2,128)(2,1)S(1)}, u32[]{:S(2)}, u32[]{:S(2)}) async-start(bf16[8,2,4096]{2,1,0:T(2,128)(2,1)} %reshape.81), calls=%async_computation.8 | async-start | bytes 262144 | tf_op jit(solution)/shard_map/all_to_all | solution.py:115
  383.5 4.5 %fusion = bf16[1,224,4096]{2,1,0:T(8,128)(2,1)} fusion(bf16[512,224]{0,1:T(8,128)(2,1)S(1)} %get-tuple-element.13, bf16[512,4096]{1,0:T(8,128)(2,1)} %reshape_reshape.3), kind=kOutput, calls=%fused_computation.7 | convolution fusion | flops 940441600 | bytes 6258688 | tf_op jit(solution)/shard_map/dot_general | solution.py:104
  388.8 0.8 convolution_convert_fusion.5
  (37 shorter events, 7.5 us)
Async XLA Ops:
  7.2 157.3 %copy-start = (bf16[1,224,4096]{2,1,0:T(8,128)(2,1)S(1)}, bf16[1,224,4096]{2,1,0:T(8,128)(2,1)}, u32[]{:S(2)}) copy-start(bf16[1,224,4096]{2,1,0:T(8,128)(2,1)} %param.12) | copy-start | bytes 5505028
  10.4 11.7 %all-to-all-start.1 = ((bf16[8,2,4096]{2,1,0:T(2,128)(2,1)}), bf16[8,2,4096]{2,1,0:T(2,128)(2,1)S(1)}, u32[]{:S(2)}, u32[]{:S(2)}) async-start(bf16[8,2,4096]{2,1,0:T(2,128)(2,1)} %reshape.80), calls=%async_computation.1 | async-start | bytes 262144 | tf_op jit(solution)/shard_map/all_to_all | solution.py:65
  37.5 115.4 %all-to-all-start.2 = ((bf16[32,8,2,4096]{3,2,1,0:T(2,128)(2,1)}), bf16[32,8,2,4096]{3,2,1,0:T(2,128)(2,1)}, u32[]{:S(2)}, u32[]{:S(2)}) async-start(bf16[32,8,2,4096]{3,2,1,0:T(2,128)(2,1)} %stack.2), calls=%async_computation.2 | async-start | bytes 8388608 | tf_op jit(solution)/shard_map/all_to_all | solution.py:73
  48.1 119.4 %all-gather.3.cloned.1.call-start = ((), (), s32[]{:S(2)}) async-start(), calls=%async_computation.9 | async-start | bytes 4325376 | tf_op jit(solution)/shard_map/all_gather | solution.py:75
  160.1 4.4 %copy-start.1 = (bf16[512,4096]{1,0:T(8,128)(2,1)S(1)}, bf16[512,4096]{1,0:T(8,128)(2,1)}, u32[]{:S(2)}) copy-start(bf16[512,4096]{1,0:T(8,128)(2,1)} %reshape_reshape.3) | copy-start | bytes 12582916
  175.1 34.7 %copy-start.3 = (f32[6,2]{0,1:T(2,128)S(1)}, f32[6,2]{0,1:T(2,128)}, u32[]{:S(2)}) copy-start(f32[6,2]{0,1:T(2,128)} %param.10) | copy-start | bytes 148
  204.4 10.0 %all-to-all-start.4 = ((f32[8,1,2]{2,1,0:T(1,128)}), f32[8,1,2]{2,1,0:T(1,128)S(1)}, u32[]{:S(2)}, u32[]{:S(2)}) async-start(f32[8,1,2]{2,1,0:T(1,128)} %bitcast.4), calls=%async_computation.4 | async-start | bytes 8192 | tf_op jit(solution)/shard_map/all_to_all | solution.py:91
  209.8 125.7 %reduce-scatter.3.cloned.1.call-start = ((), (), s32[]{:S(2)}) async-start(), calls=%async_computation.10 | async-start | bytes 5242880 | tf_op jit(solution)/shard_map/reduce_scatter | solution.py:26
  272.4 4.4 %copy-start.2 = (bf16[1,224,4096]{2,1,0:T(8,128)(2,1)S(1)}, bf16[1,224,4096]{2,1,0:T(8,128)(2,1)}, u32[]{:S(2)}) copy-start(bf16[1,224,4096]{2,1,0:T(8,128)(2,1)} %param.11) | copy-start | bytes 5505028
  281.5 90.8 %reduce-scatter.5.cloned.1.call-start = ((), (), s32[]{:S(2)}) async-start(), calls=%async_computation.11 | async-start | bytes 1179648 | tf_op jit(solution)/shard_map/reduce_scatter | solution.py:26
  374.0 14.8 %all-to-all-start.6 = ((bf16[8,2,4096]{2,1,0:T(2,128)(2,1)}), bf16[8,2,4096]{2,1,0:T(2,128)(2,1)S(1)}, u32[]{:S(2)}, u32[]{:S(2)}) async-start(bf16[8,2,4096]{2,1,0:T(2,128)(2,1)} %reshape.81), calls=%async_computation.8 | async-start | bytes 262144 | tf_op jit(solution)/shard_map/all_to_all | solution.py:115
Sparse Core Ops, SparseCore 0:
  51.5 115.9 all-gather.2
  281.7 53.7 reduce-scatter.2
  338.0 34.2 reduce-scatter.4
